TPU v7x, 128 devices: a whole 4x4x4 slice. The times are simulated.
128 devices in a mesh: seq: 16 (over z_hi, y, core), head: 8 (over x, z_lo).
Axes of the slice: x: 4, y: 4, z: 4 (z_hi: 2, z_lo: 2; z = z_hi * 2 + z_lo), core: 2. Of those that a mesh axis runs over, the one named last changes fastest.
Arguments:
- latent: bfloat16 [16, 1024, 2048], P('seq', None, 'head'), may hold values from -6 to 6
- modulation: float32 [9, 2048], replicated, may hold values from -3 to 3
- spatial_qkv: bfloat16 [3, 2048, 2048], P(None, None, 'head')
- spatial_out: bfloat16 [2048, 2048], P('head'), may hold values from -0.125 to 0.125
- temporal_qkv: bfloat16 [3, 2048, 2048], P(None, None, 'head')
- temporal_out: bfloat16 [2048, 2048], P('head'), may hold values from -0.125 to 0.125
- hidden_weight: bfloat16 [2048, 8192], P(None, 'head'), may hold values from -0.125 to 0.125
- output_weight: bfloat16 [8192, 2048], P('head'), may hold values from -0.0625 to 0.0625
Outputs:
- block_out: bfloat16 [16, 1024, 2048], P(None, 'seq', 'head')
All inputs are finite; a program needn't handle non-finite values.
Results may differ from a plain program's by a relative error of at most 0.009.
Values may be sent and summed in bfloat16 or wider, within the bound.
A program may use at most 128 MiB of HBM per device.

v0:
```python
import jax
import jax.numpy as jnp
from jax import lax
from jax.sharding import PartitionSpec as P

HD = 64


def split_up(shard, dim, devices):
    lengths = shard.shape
    blocks = shard.reshape(*lengths[:dim], devices, lengths[dim] // devices, *lengths[dim + 1 :])
    return jnp.moveaxis(blocks, dim, 0)


def sum_at_owner(shard, axis, dim):
    devices = lax.axis_size(axis)
    blocks = lax.all_to_all(split_up(shard, dim, devices), axis, 0, 0, tiled=True)
    return jnp.sum(blocks.astype(jnp.float32), axis=0)


def layer_norm(values):
    average = jnp.mean(values, axis=-1, keepdims=True)
    centred = values - average
    variance = jnp.mean(centred * centred, axis=-1, keepdims=True)
    return centred * lax.rsqrt(variance + 1e-06)


def modulate(stream, modulation, offset):
    normed = layer_norm(stream.astype(jnp.float32))
    return (normed * (1.0 + modulation[offset + 1]) + modulation[offset]).astype(jnp.bfloat16)


def attend(query, keys, values):
    scores = jnp.einsum(
        "glhd,gmhd->ghlm", query, keys, preferred_element_type=jnp.float32
    ) * HD ** (-0.5)
    attn_weights = jax.nn.softmax(scores, axis=-1).astype(jnp.bfloat16)
    return jnp.einsum(
        "ghlm,gmhd->glhd", attn_weights, values, preferred_element_type=jnp.float32
    ).astype(jnp.bfloat16)


def project_three(normed, weights):
    return [
        jnp.dot(normed, weights[member], preferred_element_type=jnp.float32).astype(jnp.bfloat16)
        for member in range(3)
    ]


def column_adder(columns, portion):
    return jnp.dot(portion, columns, preferred_element_type=jnp.float32)


def per_device(
    latent,
    modulation,
    spatial_qkv,
    spatial_out,
    temporal_qkv,
    temporal_out,
    hidden_weight,
    output_weight,
):
    width_local = latent.shape[2]
    heads_local = width_local // HD
    anchor = lax.axis_index("head") * width_local
    local_rows = lax.dynamic_slice_in_dim(modulation, anchor, width_local, 1)
    full_spatial = lax.all_gather(latent, "head", axis=2, tiled=True)
    normed = modulate(full_spatial, modulation, 0)
    frames_local = latent.shape[0]
    patches = latent.shape[1]
    query, keys, values = [
        member.reshape(frames_local, patches, heads_local, HD)
        for member in project_three(normed, spatial_qkv)
    ]
    spatial = lax.map(
        lambda triple: attend(triple[0][None], triple[1][None], triple[2][None])[0],
        (query, keys, values),
    )
    spatial = spatial.reshape(frames_local, patches, width_local)
    columns = lax.all_to_all(spatial_out, "head", split_axis=1, concat_axis=0, tiled=True)
    reduced = column_adder(columns, lax.all_gather(spatial, "head", axis=2, tiled=True))
    stream_one = (latent.astype(jnp.float32) + local_rows[2] * reduced).astype(jnp.bfloat16)
    stream_temporal = lax.all_to_all(stream_one, "seq", split_axis=1, concat_axis=0, tiled=True)
    full_temporal = lax.all_gather(stream_temporal, "head", axis=2, tiled=True)
    normed = modulate(full_temporal, modulation, 3)
    query, keys, values = project_three(normed, temporal_qkv)
    frames = stream_temporal.shape[0]
    patches_local = stream_temporal.shape[1]

    def to_groups(tensor):
        return jnp.transpose(tensor.reshape(frames, patches_local, heads_local, HD), (1, 0, 2, 3))

    temporal = attend(to_groups(query), to_groups(keys), to_groups(values))
    temporal = jnp.transpose(temporal, (1, 0, 2, 3)).reshape(frames, patches_local, width_local)
    columns = lax.all_to_all(temporal_out, "head", split_axis=1, concat_axis=0, tiled=True)
    reduced = column_adder(columns, lax.all_gather(temporal, "head", axis=2, tiled=True))
    stream_two = (stream_temporal.astype(jnp.float32) + local_rows[5] * reduced).astype(
        jnp.bfloat16
    )
    full_two = lax.all_gather(stream_two, "head", axis=2, tiled=True)
    normed = modulate(full_two, modulation, 6)
    pre_act = jnp.dot(normed, hidden_weight, preferred_element_type=jnp.float32)
    hidden = jax.nn.gelu(pre_act, approximate=True).astype(jnp.bfloat16)
    partial_sums = jnp.dot(hidden, output_weight, preferred_element_type=jnp.float32)
    reduced = sum_at_owner(partial_sums.astype(jnp.bfloat16), "head", 2)
    return (stream_two.astype(jnp.float32) + local_rows[8] * reduced).astype(jnp.bfloat16)


def solution(mesh):
    in_specs = (
        P("seq", None, "head"),
        P(),
        P(None, None, "head"),
        P("head", None),
        P(None, None, "head"),
        P("head", None),
        P(None, "head"),
        P("head", None),
    )
    out_specs = P(None, "seq", "head")
    return jax.shard_map(
        per_device, mesh=mesh, in_specs=in_specs, out_specs=out_specs, check_vma=False
    )
```

profile of v0, /device:TPU:8, one launch (start us, length us, event | category | flops | bytes accessed | tf_op | source)
XLA Modules:
  0.0 685.8 jit_solution(7628114898617417352)
XLA Ops:
  6.5 0.7 all-gather.6.cloned.1.call-update
  7.3 1.1 slice_add_fusion
  8.4 99.1 %all-gather.6.cloned.1.call-done = bf16[1,1024,2048]{2,1,0:T(8,128)(2,1)} async-done(((bf16[1,1024,256]{2,1,0:T(8,128)(2,1)}), bf16[1,1024,2048]{2,1,0:T(8,128)(2,1)}) %all-gather.6.cloned.1.call-update) | async-done | bytes 4194320 | tf_op jit(solution)/shard_map/all_gather | solution.py:68
  107.6 3.0 convert_reduce_fusion.2
  110.5 0.5 copy-done
  111.0 1.2 fusion.19
  112.3 1.9 fusion.33
  114.2 1.3 convolution_convert_fusion.6
  115.5 1.3 convolution_convert_fusion.5
  116.8 1.3 convolution_convert_fusion.4
  118.1 5.2 fusion.130
  123.3 8.1 %fusion.136 = f32[4,1024,1024]{1,2,0:T(8,128)} fusion(bf16[1024,4,64]{0,2,1:T(8,128)(2,1)S(1)} %bitcast.142, bf16[1024,4,64]{0,2,1:T(8,128)(2,1)S(1)} %bitcast.144), kind=kOutput, calls=%fused_computation.124 | convolution fusion | flops 536870912 | bytes 17825792 | tf_op jit(solution)/shard_map/while/body/eval_jaxpr/glhd,gmhd->ghlm/dot_general | solution.py:34
  131.4 16.0 %fusion.69 = bf16[4,64,1024]{2,1,0:T(8,128)(2,1)} fusion(bf16[1024,4,64]{0,2,1:T(8,128)(2,1)S(1)} %bitcast.162, f32[4,1024]{1,0:T(4,128)S(1)} %fusion.130, f32[4,1024,1024]{1,2,0:T(8,128)} %fusion.136), kind=kOutput, calls=%fused_computation.78 | convolution fusion | flops 558109696 | bytes 17842176 | tf_op jit(solution)/shard_map/while/body/eval_jaxpr/ghlm,gmhd->glhd/dot_general | solution.py:38
  147.4 1.3 copy.43
  148.7 6.0 all-to-all-start
  154.8 0.9 fusion.129
  155.6 21.3 %all-to-all-done = bf16[256,8,256]{0,2,1:T(8,128)(2,1)S(1)} async-done(((bf16[256,8,256]{0,2,1:T(8,128)(2,1)}), bf16[256,8,256]{0,2,1:T(8,128)(2,1)S(1)}, u32[]{:S(2)}, u32[]{:S(2)}) %all-to-all-start) | async-done | bytes 1048608 | tf_op jit(solution)/shard_map/all_to_all | solution.py:81
  177.0 0.5 copy.44
  177.5 71.1 %all-gather.8.cloned.1.call-done = bf16[1,1024,2048]{1,2,0:T(8,128)(2,1)} async-done(((bf16[1,1024,256]{1,2,0:T(8,128)(2,1)}), bf16[1,1024,2048]{1,2,0:T(8,128)(2,1)}) %all-gather.8.cloned.1.call-update) | async-done | bytes 4194320 | tf_op jit(solution)/shard_map/all_gather | solution.py:82
  248.6 3.5 fusion.65
  252.1 0.8 copy.91
  252.9 0.5 broadcast.127
  253.4 3.8 reduce.6
  257.4 15.9 %all_to_all.55 = bf16[16,2,8192]{2,1,0:T(2,128)(2,1)S(1)} all-to-all(bf16[16,2,8192]{2,1,0:T(2,128)(2,1)S(1)} %reshape.181), channel_id=1, replica_groups=mesh['seq'=16,'head'=8] {'seq'}, dimensions={0} | all-to-all | bytes 1048576 | tf_op jit(solution)/shard_map/all_to_all | solution.py:84
  273.2 0.5 reshape.182
  273.8 0.9 copy.55
  274.9 94.6 %all-gather.10.cloned.1.call-done = bf16[16,64,2048]{2,1,0:T(8,128)(2,1)} async-done(((bf16[16,64,256]{2,1,0:T(8,128)(2,1)}), bf16[16,64,2048]{2,1,0:T(8,128)(2,1)}) %all-gather.10.cloned.1.call-update) | async-done | bytes 4194320 | tf_op jit(solution)/shard_map/all_gather | solution.py:85
  369.5 3.0 convert_reduce_fusion.1
  372.9 1.2 fusion.15
  374.2 3.0 convolution_convert_fusion.1
  377.5 4.2 convolution_convert_fusion.2
  382.2 5.0 convolution_convert_fusion.3
  387.2 2.2 reshape.170
  389.4 3.3 fusion.131
  392.7 2.5 fusion.54
  395.2 0.5 copy.50
  395.7 1.5 reshape.173
  397.4 24.8 %all_to_all.56 = bf16[256,8,256]{2,0,1:T(8,128)(2,1)S(1)} all-to-all(bf16[256,8,256]{2,0,1:T(8,128)(2,1)S(1)} %bitcast.138), channel_id=1, replica_groups=mesh['seq'=16,'head'=8] {'head'}, dimensions={1} | all-to-all | bytes 2097152 | tf_op jit(solution)/shard_map/all_to_all | solution.py:96
  422.2 74.8 %all-gather.12.cloned.1.call-done = bf16[16,64,2048]{2,1,0:T(8,128)(2,1)} async-done(((bf16[16,64,256]{2,1,0:T(8,128)(2,1)}), bf16[16,64,2048]{2,1,0:T(8,128)(2,1)}) %all-gather.12.cloned.1.call-update) | async-done | bytes 4194320 | tf_op jit(solution)/shard_map/all_gather | solution.py:97
  497.0 4.2 fusion.68
  501.3 100.4 %all-gather.14.cloned.1.call-done = bf16[16,64,2048]{2,1,0:T(8,128)(2,1)} async-done(((bf16[16,64,256]{2,1,0:T(8,128)(2,1)}), bf16[16,64,2048]{2,1,0:T(8,128)(2,1)}) %all-gather.14.cloned.1.call-update) | async-done | bytes 4194320 | tf_op jit(solution)/shard_map/all_gather | solution.py:101
  601.7 3.0 convert_reduce_fusion
  605.2 1.2 fusion.11
  606.4 15.3 %fusion.45 = bf16[16,64,2048]{2,1,0:T(8,128)(2,1)} fusion(bf16[1024,2048]{1,0:T(8,128)(2,1)} %param.15, bf16[16,64,2048]{2,1,0:T(8,128)(2,1)} %all-gather.14.cloned.1.call-done, bf16[2048,1024]{1,0:T(8,128)(2,1)} %param.14, f32[2048]{0:T(1024)S(1)} %bitcast.152, f32[2048]{0:T(1024)S(1)} %bitcast.151, f32[16,64]{1,0:T(8,128)S(1)} %add_rsqrt_fusion, ...), kind=kOutput, calls=%fused_computation.54 | convolution fusion | flops 8614051840 | bytes 16801792 | tf_op jit(solution)/shard_map/dot_general | solution.py:105
  621.7 2.8 copy.89
  624.5 52.6 %all_to_all.57 = bf16[8,16,64,256]{3,2,1,0:T(8,128)(2,1)S(1)} all-to-all(bf16[8,16,64,256]{3,2,1,0:T(8,128)(2,1)S(1)} %bitcast.133), channel_id=1, replica_groups=mesh['seq'=16,'head'=8] {'head'}, dimensions={0} | all-to-all | bytes 8388608 | tf_op jit(solution)/shard_map/all_to_all | solution.py:17
  677.1 0.7 convert_reduce_fusion.3
  678.1 0.9 add_convert_fusion
  (36 shorter events, 2.8 us)
Async XLA Ops:
  6.5 101.0 %all-gather.6.cloned.1.call-start = ((), (), s32[]{:S(2)}) async-start(), calls=%async_computation.4 | async-start | bytes 4718592 | tf_op jit(solution)/shard_map/all_gather | solution.py:68
  7.3 241.3 %all-gather.8.cloned.1.call-start = ((), (), s32[]{:S(2)}) async-start(), calls=%async_computation.5 | async-start | bytes 4718592 | tf_op jit(solution)/shard_map/all_gather | solution.py:82
  107.6 3.4 copy-start
  112.3 1.9 copy-start.8
  131.4 16.0 %copy-start.5 = (bf16[256,2048]{1,0:T(8,128)(2,1)S(1)}, bf16[256,2048]{1,0:T(8,128)(2,1)}, u32[]{:S(2)}) copy-start(bf16[256,2048]{1,0:T(8,128)(2,1)} %param.11) | copy-start | bytes 3145732
  147.4 101.2 %copy-start.7 = (bf16[1,1024,256]{2,1,0:T(8,128)(2,1)S(1)}, bf16[1,1024,256]{2,1,0:T(8,128)(2,1)}, u32[]{:S(2)}) copy-start(bf16[1,1024,256]{2,1,0:T(8,128)(2,1)} %param.8) | copy-start | bytes 1572868
  148.7 28.2 %all-to-all-start = ((bf16[256,8,256]{0,2,1:T(8,128)(2,1)}), bf16[256,8,256]{0,2,1:T(8,128)(2,1)S(1)}, u32[]{:S(2)}, u32[]{:S(2)}) async-start(bf16[256,8,256]{0,2,1:T(8,128)(2,1)} %bitcast.14), calls=%async_computation | async-start | bytes 2097152 | tf_op jit(solution)/shard_map/all_to_all | solution.py:81
  154.7 214.7 %all-gather.10.cloned.1.call-start = ((), (), s32[]{:S(2)}) async-start(), calls=%async_computation.6 | async-start | bytes 4718592 | tf_op jit(solution)/shard_map/all_gather | solution.py:85
  274.7 222.4 %all-gather.12.cloned.1.call-start = ((), (), s32[]{:S(2)}) async-start(), calls=%async_computation.7 | async-start | bytes 4718592 | tf_op jit(solution)/shard_map/all_gather | solution.py:97
  369.5 3.4 copy-start.1
  395.2 2.1 copy-start.6
  395.2 101.8 %copy-start.3 = (bf16[1,1024,256]{2,1,0:T(8,128)(2,1)S(1)}, bf16[1,1024,256]{2,1,0:T(8,128)(2,1)}, u32[]{:S(2)}) copy-start(bf16[1,1024,256]{2,1,0:T(8,128)(2,1)} %copy.55) | copy-start | bytes 1572868
  397.2 204.5 %all-gather.14.cloned.1.call-start = ((), (), s32[]{:S(2)}) async-start(), calls=%async_computation.8 | async-start | bytes 4718592 | tf_op jit(solution)/shard_map/all_gather | solution.py:101
  601.7 3.4 copy-start.2
  677.1 1.0 copy-start.4
Sparse Core Ops, SparseCore 0:
  8.9 98.6 all-gather.5
  147.5 101.0 all-gather.7
  274.8 94.6 all-gather.9
  397.3 99.6 all-gather.11
  501.4 100.2 all-gather.13
where the time goes:
time: 696 us; the launch traced here: 686 us
  waiting for transfers between devices  462 us (66%)
  blocking collectives  93.3 us (13%)
  matrix products  74.2 us (11%)
  other arithmetic  21.1 us (3%)
  local copies, waits for them, and re-layouts  15.2 us (2%)
  between operations  13.6 us (2%)
    all_gather x1, waiting for transfers between devices, per_device(): full_two = lax.all_gather(stream_two, 'head', axis=2, tiled=True)  100 us
    all_gather x1, waiting for transfers between devices, per_device(): full_spatial = lax.all_gather(latent, 'head', axis=2, tiled=True)  99.1 us
    all_gather x1, waiting for transfers between devices, per_device(): full_temporal = lax.all_gather(stream_temporal, 'head', axis=2, tiled=True)  94.6 us
    all_gather x1, waiting for transfers between devices, per_device(): lax.all_gather(temporal, 'head', axis=2, tiled=True)  74.8 us
    all_gather x1, waiting for transfers between devices, per_device(): lax.all_gather(spatial, 'head', axis=2, tiled=True)  71.1 us
    all_to_all x1, blocking collectives, sum_at_owner(): lax.all_to_all(split_up(shard, dim, devices), axis, 0, 0, tiled=True)  52.6 us
    all_to_all x1, blocking collectives, per_device(): lax.all_to_all(temporal_out, 'head', split_axis=1, concat_axis=0, tiled=T...  24.8 us
    all_to_all x1, waiting for transfers between devices, per_device(): lax.all_to_all(spatial_out, 'head', split_axis=1, concat_axis=0, tiled=True)  21.3 us
  transfers between devices with their start and end apart: 6, of which 6 were waited for; matrix products, arithmetic and copies ran while one was open for 1% of the time, Pallas kernels for 0%

commit v1 on v0

--- a/solution.py
+++ b/solution.py
@@ -79,7 +79,7 @@
     )
     spatial = spatial.reshape(frames_local, patches, width_local)
     columns = lax.all_to_all(spatial_out, "head", split_axis=1, concat_axis=0, tiled=True)
-    reduced = column_adder(columns, lax.all_gather(spatial, "head", axis=2, tiled=True))
+    reduced = column_adder(columns, jnp.concatenate(lax.all_gather(spatial, "head"), axis=2))
     stream_one = (latent.astype(jnp.float32) + local_rows[2] * reduced).astype(jnp.bfloat16)
     stream_temporal = lax.all_to_all(stream_one, "seq", split_axis=1, concat_axis=0, tiled=True)
     full_temporal = lax.all_gather(stream_temporal, "head", axis=2, tiled=True)

time: 696 us -> 703 us (1.010)
  local copies, waits for them, and re-layouts: 15.2 us -> 23.1 us
where the time goes in v1:
time: 703 us; the launch traced here: 693 us
  waiting for transfers between devices  462 us (66%)
  blocking collectives  93.3 us (13%)
  matrix products  73.5 us (10%)
  local copies, waits for them, and re-layouts  23.1 us (3%)
  other arithmetic  21.1 us (3%)
  between operations  13.7 us (2%)
    all_gather x1, waiting for transfers between devices, per_device(): full_two = lax.all_gather(stream_two, 'head', axis=2, tiled=True)  100 us
    all_gather x1, waiting for transfers between devices, per_device(): full_spatial = lax.all_gather(latent, 'head', axis=2, tiled=True)  99.1 us
    all_gather x1, waiting for transfers between devices, per_device(): full_temporal = lax.all_gather(stream_temporal, 'head', axis=2, tiled=True)  94.6 us
    all_gather x1, waiting for transfers between devices, per_device(): lax.all_gather(temporal, 'head', axis=2, tiled=True)  74.8 us
    all_gather x1, waiting for transfers between devices, per_device(): lax.all_gather(spatial, 'head')  71.1 us
    all_to_all x1, blocking collectives, sum_at_owner(): lax.all_to_all(split_up(shard, dim, devices), axis, 0, 0, tiled=True)  52.6 us
    all_to_all x1, blocking collectives, per_device(): lax.all_to_all(temporal_out, 'head', split_axis=1, concat_axis=0, tiled=T...  24.9 us
    all_to_all x1, waiting for transfers between devices, per_device(): lax.all_to_all(spatial_out, 'head', split_axis=1, concat_axis=0, tiled=True)  21.3 us
  transfers between devices with their start and end apart: 6, of which 6 were waited for; matrix products, arithmetic and copies ran while one was open for 1% of the time, Pallas kernels for 0%

profile of v1, /device:TPU:8, one launch (start us, length us, event | category | flops | bytes accessed | tf_op | source)
XLA Modules:
  0.0 692.6 jit_solution(3294920829588243222)
XLA Ops:
  6.5 0.7 all-gather.6.cloned.1.call-update
  7.3 1.1 slice_add_fusion
  8.4 99.1 %all-gather.6.cloned.1.call-done = bf16[1,1024,2048]{2,1,0:T(8,128)(2,1)} async-done(((bf16[1,1024,256]{2,1,0:T(8,128)(2,1)}), bf16[1,1024,2048]{2,1,0:T(8,128)(2,1)}) %all-gather.6.cloned.1.call-update) | async-done | bytes 4194320 | tf_op jit(solution)/shard_map/all_gather | solution.py:68
  107.6 3.0 convert_reduce_fusion.2
  111.0 1.2 fusion.19
  112.3 1.9 fusion.33
  114.2 1.3 convolution_convert_fusion.6
  115.5 1.3 convolution_convert_fusion.5
  116.8 1.3 convolution_convert_fusion.4
  118.1 5.2 fusion.119
  123.3 8.1 %fusion.125 = f32[4,1024,1024]{1,2,0:T(8,128)} fusion(bf16[1024,4,64]{0,2,1:T(8,128)(2,1)S(1)} %bitcast.136, bf16[1024,4,64]{0,2,1:T(8,128)(2,1)S(1)} %bitcast.138), kind=kOutput, calls=%fused_computation.122 | convolution fusion | flops 536870912 | bytes 17825792 | tf_op jit(solution)/shard_map/while/body/eval_jaxpr/glhd,gmhd->ghlm/dot_general | solution.py:34
  131.4 15.3 %fusion.58 = bf16[4,64,1024]{2,1,0:T(8,128)(2,1)S(1)} fusion(bf16[1024,4,64]{0,2,1:T(8,128)(2,1)S(1)} %bitcast.156, f32[4,1024]{1,0:T(4,128)S(1)} %fusion.119, f32[4,1024,1024]{1,2,0:T(8,128)} %fusion.125), kind=kOutput, calls=%fused_computation.76 | convolution fusion | flops 558109696 | bytes 17842176 | tf_op jit(solution)/shard_map/while/body/eval_jaxpr/ghlm,gmhd->glhd/dot_general | solution.py:38
  146.7 1.0 copy.44
  147.7 1.8 copy.46
  149.5 5.5 all-to-all-start
  155.1 0.9 fusion.118
  155.9 21.3 %all-to-all-done = bf16[256,8,256]{0,2,1:T(8,128)(2,1)S(1)} async-done(((bf16[256,8,256]{0,2,1:T(8,128)(2,1)}), bf16[256,8,256]{0,2,1:T(8,128)(2,1)S(1)}, u32[]{:S(2)}, u32[]{:S(2)}) %all-to-all-start) | async-done | bytes 1048608 | tf_op jit(solution)/shard_map/all_to_all | solution.py:81
  177.3 0.5 copy.47
  177.8 71.1 %all-gather.8.cloned.1.call-done = bf16[8,1,1024,256]{3,2,1,0:T(8,128)(2,1)} async-done(((bf16[1,1,1024,256]{3,2,1,0:T(8,128)(2,1)}), bf16[8,1,1024,256]{3,2,1,0:T(8,128)(2,1)}) %all-gather.8.cloned.1.call-update) | async-done | bytes 4194320 | tf_op jit(solution)/shard_map/all_gather | solution.py:82
  248.9 6.5 copy.45
  255.4 3.5 fusion.57
  258.9 0.8 copy.94
  259.7 0.5 broadcast.127
  260.2 3.8 reduce.6
  264.1 15.9 %all_to_all.55 = bf16[16,2,8192]{2,1,0:T(2,128)(2,1)S(1)} all-to-all(bf16[16,2,8192]{2,1,0:T(2,128)(2,1)S(1)} %reshape.183), channel_id=1, replica_groups=mesh['seq'=16,'head'=8] {'seq'}, dimensions={0} | all-to-all | bytes 1048576 | tf_op jit(solution)/shard_map/all_to_all | solution.py:84
  280.0 0.5 reshape.184
  280.5 0.9 copy.58
  281.6 94.6 %all-gather.10.cloned.1.call-done = bf16[16,64,2048]{2,1,0:T(8,128)(2,1)} async-done(((bf16[16,64,256]{2,1,0:T(8,128)(2,1)}), bf16[16,64,2048]{2,1,0:T(8,128)(2,1)}) %all-gather.10.cloned.1.call-update) | async-done | bytes 4194320 | tf_op jit(solution)/shard_map/all_gather | solution.py:85
  376.2 3.0 convert_reduce_fusion.1
  379.7 1.2 fusion.15
  380.9 3.0 convolution_convert_fusion.1
  384.3 4.2 convolution_convert_fusion.2
  388.9 5.0 convolution_convert_fusion.3
  393.9 2.2 reshape.172
  396.2 3.3 fusion.120
  399.5 2.5 fusion.52
  402.5 1.5 reshape.175
  404.1 24.9 %all_to_all.56 = bf16[256,8,256]{2,0,1:T(8,128)(2,1)S(1)} all-to-all(bf16[256,8,256]{2,0,1:T(8,128)(2,1)S(1)} %bitcast.132), channel_id=1, replica_groups=mesh['seq'=16,'head'=8] {'head'}, dimensions={1} | all-to-all | bytes 2097152 | tf_op jit(solution)/shard_map/all_to_all | solution.py:96
  429.0 74.8 %all-gather.12.cloned.1.call-done = bf16[16,64,2048]{2,1,0:T(8,128)(2,1)} async-done(((bf16[16,64,256]{2,1,0:T(8,128)(2,1)}), bf16[16,64,2048]{2,1,0:T(8,128)(2,1)}) %all-gather.12.cloned.1.call-update) | async-done | bytes 4194320 | tf_op jit(solution)/shard_map/all_gather | solution.py:97
  503.8 4.2 fusion.56
  508.1 100.4 %all-gather.14.cloned.1.call-done = bf16[16,64,2048]{2,1,0:T(8,128)(2,1)} async-done(((bf16[16,64,256]{2,1,0:T(8,128)(2,1)}), bf16[16,64,2048]{2,1,0:T(8,128)(2,1)}) %all-gather.14.cloned.1.call-update) | async-done | bytes 4194320 | tf_op jit(solution)/shard_map/all_gather | solution.py:101
  608.5 3.0 convert_reduce_fusion
  611.9 1.2 fusion.11
  613.2 15.3 %fusion.43 = bf16[16,64,2048]{2,1,0:T(8,128)(2,1)} fusion(bf16[1024,2048]{1,0:T(8,128)(2,1)} %param.15, bf16[16,64,2048]{2,1,0:T(8,128)(2,1)} %all-gather.14.cloned.1.call-done, bf16[2048,1024]{1,0:T(8,128)(2,1)} %param.14, f32[2048]{0:T(1024)S(1)} %bitcast.146, f32[2048]{0:T(1024)S(1)} %bitcast.145, f32[16,64]{1,0:T(8,128)S(1)} %add_rsqrt_fusion, ...), kind=kOutput, calls=%fused_computation.52 | convolution fusion | flops 8614051840 | bytes 16801792 | tf_op jit(solution)/shard_map/dot_general | solution.py:105
  628.5 2.8 copy.92
  631.2 52.6 %all_to_all.57 = bf16[8,16,64,256]{3,2,1,0:T(8,128)(2,1)S(1)} all-to-all(bf16[8,16,64,256]{3,2,1,0:T(8,128)(2,1)S(1)} %bitcast.126), channel_id=1, replica_groups=mesh['seq'=16,'head'=8] {'head'}, dimensions={0} | all-to-all | bytes 8388608 | tf_op jit(solution)/shard_map/all_to_all | solution.py:17
  683.8 0.7 convert_reduce_fusion.3
  684.8 0.9 add_convert_fusion
  (38 shorter events, 3.7 us)
Async XLA Ops:
  6.5 101.0 %all-gather.6.cloned.1.call-start = ((), (), s32[]{:S(2)}) async-start(), calls=%async_computation.4 | async-start | bytes 4718592 | tf_op jit(solution)/shard_map/all_gather | solution.py:68
  7.3 241.6 %all-gather.8.cloned.1.call-start = ((), (), s32[]{:S(2)}) async-start(), calls=%async_computation.5 | async-start | bytes 4718592 | tf_op jit(solution)/shard_map/all_gather | solution.py:82
  107.6 3.4 copy-start
  112.3 1.9 copy-start.8
  131.4 16.3 %copy-start.5 = (bf16[256,2048]{1,0:T(8,128)(2,1)S(1)}, bf16[256,2048]{1,0:T(8,128)(2,1)}, u32[]{:S(2)}) copy-start(bf16[256,2048]{1,0:T(8,128)(2,1)} %param.11) | copy-start | bytes 3145732
  149.5 27.7 %all-to-all-start = ((bf16[256,8,256]{0,2,1:T(8,128)(2,1)}), bf16[256,8,256]{0,2,1:T(8,128)(2,1)S(1)}, u32[]{:S(2)}, u32[]{:S(2)}) async-start(bf16[256,8,256]{0,2,1:T(8,128)(2,1)} %bitcast.15), calls=%async_computation | async-start | bytes 2097152 | tf_op jit(solution)/shard_map/all_to_all | solution.py:81
  155.0 221.2 %all-gather.10.cloned.1.call-start = ((), (), s32[]{:S(2)}) async-start(), calls=%async_computation.6 | async-start | bytes 4718592 | tf_op jit(solution)/shard_map/all_gather | solution.py:85
  177.8 77.6 %copy-start.7 = (bf16[1,1024,256]{2,1,0:T(8,128)(2,1)S(1)}, bf16[1,1024,256]{2,1,0:T(8,128)(2,1)}, u32[]{:S(2)}) copy-start(bf16[1,1024,256]{2,1,0:T(8,128)(2,1)} %param.8) | copy-start | bytes 1572868
  281.4 222.4 %all-gather.12.cloned.1.call-start = ((), (), s32[]{:S(2)}) async-start(), calls=%async_computation.7 | async-start | bytes 4718592 | tf_op jit(solution)/shard_map/all_gather | solution.py:97
  376.2 3.4 copy-start.1
  402.0 2.1 copy-start.6
  402.0 101.8 %copy-start.3 = (bf16[1,1024,256]{2,1,0:T(8,128)(2,1)S(1)}, bf16[1,1024,256]{2,1,0:T(8,128)(2,1)}, u32[]{:S(2)}) copy-start(bf16[1,1024,256]{2,1,0:T(8,128)(2,1)} %copy.58) | copy-start | bytes 1572868
  404.0 204.5 %all-gather.14.cloned.1.call-start = ((), (), s32[]{:S(2)}) async-start(), calls=%async_computation.8 | async-start | bytes 4718592 | tf_op jit(solution)/shard_map/all_gather | solution.py:101
  608.5 3.4 copy-start.2
  683.8 1.0 copy-start.4
Sparse Core Ops, SparseCore 0:
  8.9 98.6 all-gather.5
  147.8 101.0 all-gather.7
  281.5 94.6 all-gather.9
  404.1 99.6 all-gather.11
  508.2 100.2 all-gather.13
